TPU v7x, 32 devices: a whole 2x2x4 slice. The times are simulated.
32 devices in a mesh: mem: 4 (over y, core), tile: 8 (over z, x).
Axes of the slice: x: 2, y: 2, z: 4, core: 2. Of those that a mesh axis runs over, the one named last changes fastest.
Arguments:
- ensemble_profiles_before: bfloat16 [64, 40, 4096], P('mem', None, 'tile'), may hold values from -6 to 6
- mixing_coefficient: float32 [4096], P('tile'), may hold values from 0.05 to 0.24
- surface_driver: float32 [64, 4096], P('mem', 'tile'), may hold values from -3 to 3
- terrain_indicator: int32 [4096], P('tile'), may hold values 0 or 1
- measured_profile_position: int32 [32768], P('tile'), may hold values from 0 to 511
- measured_field_index: int32 [32768], P('tile'), may hold values from 0 to 39
- obs_valid: int32 [32768], P('tile'), may hold values 0 or 1
- obs_value: bfloat16 [32768], P('tile'), may hold values from -6 to 6
- obs_error: bfloat16 [32768], P('tile'), may hold values from 0.5 to 4
- local_weight: float32 [4, 8, 20480], P('mem', 'tile'), may hold values from 0.001 to 0.03
Outputs:
- analysis: bfloat16 [64, 40, 4096], P('mem', None, 'tile')
All inputs are finite; a program needn't handle non-finite values. No bound on the sum of `terrain_indicator` or of `obs_valid` on one device may be relied on, other than what follows from the above.
Results may differ from a plain program's by a relative error of at most 0.0034.
Values may be sent and summed in bfloat16 or wider, within the bound.
A program may use at most 64 MiB of HBM per device.

v0:
```python
import jax
import jax.numpy as jnp
from jax import lax
from jax.sharding import PartitionSpec as P

REACH = 2
NS_ITERS = 3


EXACT = lax.Precision.HIGHEST


def from_behind(value, axis, steps):
    count = lax.axis_size(axis)
    pairs = [(source, (source + steps) % count) for source in range(count)]
    return lax.ppermute(value, axis, pairs)


def vertical_mixing_step(
    ensemble_profiles_before, mixing_coefficient, surface_driver, terrain_indicator
):
    values = ensemble_profiles_before.astype(jnp.float32)
    above_layer = jnp.concatenate([values[:, :1], values[:, :-1]], axis=1)
    below_layer = jnp.concatenate([values[:, 1:], values[:, -1:]], axis=1)
    diffused = values + mixing_coefficient[None, None, :] * (
        above_layer - 2.0 * values + below_layer
    )
    stepped = diffused - 0.05 * values * values * values
    surface = jnp.concatenate([stepped[:, :1] + surface_driver[:, None, :], stepped[:, 1:]], axis=1)
    result = jnp.where(terrain_indicator[None, None, :] > 0, surface, values)
    return result.astype(jnp.bfloat16)


def measurement_operator(background_ensemble, measured_profile_position, measured_field_index):
    profile_sequence = background_ensemble.shape[2]
    unrolled_ensemble = background_ensemble.reshape(background_ensemble.shape[0], -1)
    slot_index = measured_field_index * profile_sequence + measured_profile_position
    return jnp.take(unrolled_ensemble, slot_index, axis=1)


def prepare(window):
    ensemble_profiles = window.shape[0] - 3
    measured_quantities = window[:ensemble_profiles].astype(jnp.float32)
    average = jnp.mean(measured_quantities, axis=0)
    deviation = measured_quantities - average
    innovation = window[ensemble_profiles].astype(jnp.float32) - average
    obs_precision = window[ensemble_profiles + 2].astype(jnp.float32) / window[
        ensemble_profiles + 1
    ].astype(jnp.float32)
    return (deviation, innovation, obs_precision)


def weights_for(deviation, innovation, precision, portions):
    ensemble_profiles = deviation.shape[0]
    portion_width = deviation.shape[1] // portions
    spread = jnp.zeros((ensemble_profiles, ensemble_profiles), jnp.float32)
    for portion_index in range(portions):
        portion = deviation[:, portion_index * portion_width : (portion_index + 1) * portion_width]
        scaled = (
            portion
            * precision[None, portion_index * portion_width : (portion_index + 1) * portion_width]
        )
        spread = spread + jnp.dot(
            scaled, portion.T, precision=EXACT, preferred_element_type=jnp.float32
        )
    spread = spread / (ensemble_profiles - 1.0)
    pulled = jnp.dot(
        deviation, precision * innovation, precision=EXACT, preferred_element_type=jnp.float32
    ) / (ensemble_profiles - 1.0)
    identity = jnp.eye(ensemble_profiles, dtype=jnp.float32)
    system = identity + spread
    norm_scale = jnp.sqrt(jnp.sum(system * system))

    def newton(sweep, carry):
        current, inv_root = carry
        middle = 1.5 * identity - 0.5 * jnp.dot(inv_root, current, precision=EXACT)
        return (
            jnp.dot(current, middle, precision=EXACT),
            jnp.dot(middle, inv_root, precision=EXACT),
        )

    current, inv_root = lax.fori_loop(0, NS_ITERS, newton, (system / norm_scale, identity))
    inv_root = inv_root / jnp.sqrt(norm_scale)
    inverse = jnp.dot(inv_root, inv_root, precision=EXACT)
    mean_weight = jnp.dot(inverse, pulled, precision=EXACT)
    return inv_root + mean_weight[:, None]


def update(states, transform, land_block):
    values = states.astype(jnp.float32)
    average = jnp.mean(values, axis=0)
    deviation = values - average[None]
    moved = jnp.einsum("isc,ij->jsc", deviation, transform, precision=EXACT)
    result = jnp.where(land_block[None, None, :] > 0, average[None] + moved, values)
    return result.astype(jnp.bfloat16)


def on_device(
    ensemble_profiles_before,
    mixing_coefficient,
    surface_driver,
    terrain_indicator,
    measured_profile_position,
    measured_field_index,
    obs_valid,
    obs_value,
    obs_error,
    local_weight,
):
    background_ensemble = vertical_mixing_step(
        ensemble_profiles_before, mixing_coefficient, surface_driver, terrain_indicator
    )
    measured_quantities = measurement_operator(
        background_ensemble, measured_profile_position, measured_field_index
    )
    metadata = jnp.stack([obs_value, obs_error, obs_valid.astype(jnp.bfloat16)])
    own_rows = jnp.concatenate([measured_quantities, metadata], axis=0)
    pieces = []
    for offset in range(-REACH, REACH + 1):
        if offset == 0:
            pieces.append(own_rows)
        else:
            pieces.append(from_behind(own_rows, "tile", -offset))
    nearby = jnp.concatenate(pieces, axis=1)
    members_here = measured_quantities.shape[0]
    everyone = lax.all_gather(nearby[:members_here], "mem", axis=0, tiled=True)
    window = jnp.concatenate([everyone, nearby[members_here:]], axis=0)
    regrouped_states = lax.all_to_all(
        background_ensemble, "mem", split_axis=2, concat_axis=0, tiled=True
    )
    deviation, innovation, obs_precision = prepare(window)
    columns_here = regrouped_states.shape[2]
    local_land = lax.dynamic_slice_in_dim(
        terrain_indicator, lax.axis_index("mem") * columns_here, columns_here
    )
    transform = weights_for(
        deviation, innovation, obs_precision * local_weight[0, 0], 2 * REACH + 1
    )
    outputs = update(regrouped_states, transform, local_land)
    return lax.all_to_all(outputs, "mem", split_axis=0, concat_axis=2, tiled=True)


def solution(mesh):
    in_specs = (
        P("mem", None, "tile"),
        P("tile"),
        P("mem", "tile"),
        P("tile"),
        P("tile"),
        P("tile"),
        P("tile"),
        P("tile"),
        P("tile"),
        P("mem", "tile", None),
    )
    out_specs = P("mem", None, "tile")
    return jax.shard_map(
        on_device, mesh=mesh, in_specs=in_specs, out_specs=out_specs, check_vma=False
    )
```

profile of v0, /device:TPU:1, one launch (start us, length us, event | category | flops | bytes accessed | tf_op | source)
XLA Modules:
  0.0 117.9 jit_solution(11728827272197308647)
XLA Ops:
  6.5 1.3 %copy_convert_fusion = f32[16,40,512]{2,0,1:T(8,128)S(1)} fusion(bf16[16,40,512]{2,1,0:T(8,128)(2,1)} %param.12), kind=kLoop, calls=%fused_computation.48 | loop fusion | flops 327680 | bytes 1966080 | tf_op jit(solution)/shard_map/convert_element_type | solution.py:22
  10.5 3.5 %copy.108 = bf16[16,40,512]{0,2,1:T(8,128)(2,1)} copy(bf16[16,40,512]{2,0,1:T(8,128)(2,1)S(1)} %fusion.19) | data formatting | bytes 1310720 | tf_op jit(solution)/shard_map/convert_element_type | solution.py:31
  14.0 14.2 %gather_fusion = bf16[4096,16]{1,0:T(8,128)(2,1)S(1)} fusion(bf16[16,20480]{0,1:T(8,128)(2,1)} %bitcast.68, s32[4096]{0:T(1024)S(1)} %broadcast_clamp_fusion), kind=kCustom, calls=%fused_computation | custom fusion | bytes 278528 | tf_op jit(solution)/shard_map/jit(_take)/gather | solution.py:38
  28.2 2.1 %select_bitcast_fusion = bf16[16,4096]{0,1:T(8,128)(2,1)S(1)} fusion(bf16[4096,16]{1,0:T(8,128)(2,1)S(1)} %gather_fusion, pred[4096]{0:T(1024)(128)(4,1)S(1)} %compare_and_fusion), kind=kLoop, calls=%fused_computation.45 | loop fusion | flops 65536 | bytes 266240 | tf_op jit(solution)/shard_map/jit(_take)/select_n | solution.py:38
  30.8 2.2 %collective-permute-start = (bf16[19,4096]{1,0:T(8,128)(2,1)S(1)}, bf16[19,4096]{1,0:T(8,128)(2,1)}, u32[]{:S(2)}, u32[]{:S(2)}) collective-permute-start(bf16[19,4096]{1,0:T(8,128)(2,1)S(1)} %pad_maximum_fusion), channel_id=1, source_target_pairs={{0,2},{1,3},{2,4},{3,5},{4,6},{5,7},{6,0},{7,1},{8,10},{9,11},{10,... | collective-permute-start | bytes 466952 | tf_op jit(solution)/shard_map/ppermute | solution.py:16
  33.0 1.2 %collective-permute-start.1 = (bf16[19,4096]{1,0:T(8,128)(2,1)S(1)}, bf16[19,4096]{1,0:T(8,128)(2,1)}, u32[]{:S(2)}, u32[]{:S(2)}) collective-permute-start(bf16[19,4096]{1,0:T(8,128)(2,1)S(1)} %pad_maximum_fusion), channel_id=1, source_target_pairs={{0,1},{1,2},{2,3},{3,4},{4,5},{5,6},{6,7},{7,0},{8,9},{9,10},{10,1... | collective-permute-start | bytes 466952 | tf_op jit(solution)/shard_map/ppermute | solution.py:16
  34.2 3.0 %collective-permute-start.2 = (bf16[19,4096]{1,0:T(8,128)(2,1)S(1)}, bf16[19,4096]{1,0:T(8,128)(2,1)S(1)}, u32[]{:S(2)}, u32[]{:S(2)}) collective-permute-start(bf16[19,4096]{1,0:T(8,128)(2,1)S(1)} %pad_maximum_fusion), channel_id=1, source_target_pairs={{0,7},{1,0},{2,1},{3,2},{4,3},{5,4},{6,5},{7,6},{8,15},{9,8},{10,9... | collective-permute-start | bytes 466952 | tf_op jit(solution)/shard_map/ppermute | solution.py:16
  37.4 2.3 %copy.105 = bf16[16,40,512]{1,0,2:T(8,128)(2,1)S(1)} copy(bf16[16,40,512]{2,0,1:T(8,128)(2,1)S(1)} %fusion.19) | data formatting | bytes 1310720 | tf_op jit(solution)/shard_map/convert_element_type | solution.py:31
  39.8 4.1 %reshape.54 = bf16[4,2,40960]{2,1,0:T(2,128)(2,1)} reshape(bf16[512,16,40]{2,1,0:T(8,128)(2,1)S(1)} %bitcast.67) | data formatting | bytes 1310720
  43.8 5.0 %all-to-all-start = ((bf16[4,2,40960]{2,1,0:T(2,128)(2,1)}), bf16[4,2,40960]{2,1,0:T(2,128)(2,1)S(1)}, u32[]{:S(2)}, u32[]{:S(2)}) async-start(bf16[4,2,40960]{2,1,0:T(2,128)(2,1)} %reshape.54), calls=%async_computation | async-start | bytes 1310720 | tf_op jit(solution)/shard_map/all_to_all | solution.py:128
  48.8 1.3 %dynamic-slice_compare_fusion = pred[128]{0:T(512)(128)(4,1)} fusion(s32[512]{0:T(512)} %param.15, s32[]{:T(128)S(6)} %select_n.20), kind=kLoop, calls=%fused_computation.81 | loop fusion | flops 128 | bytes 644 | tf_op jit(solution)/shard_map/gt | solution.py:94
  50.1 0.9 constant_dynamic-update-slice_fusion.4
  51.0 0.9 constant_dynamic-update-slice_fusion.3
  52.1 0.9 slice.92
  53.0 0.8 fusion.50
  53.9 4.2 %all-to-all-done = bf16[4,2,40960]{2,1,0:T(2,128)(2,1)S(1)} async-done(((bf16[4,2,40960]{2,1,0:T(2,128)(2,1)}), bf16[4,2,40960]{2,1,0:T(2,128)(2,1)S(1)}, u32[]{:S(2)}, u32[]{:S(2)}) %all-to-all-start) | async-done | bytes 655392 | tf_op jit(solution)/shard_map/all_to_all | solution.py:128
  58.0 3.2 %reshape.55 = bf16[512,16,40]{2,1,0:T(8,128)(2,1)S(1)} reshape(bf16[4,2,40960]{2,1,0:T(2,128)(2,1)S(1)} %all-to-all-done) | data formatting | bytes 1310720
  61.2 2.2 %copy.111 = f32[16,40,4,128]{3,0,2,1:T(8,128)S(1)} copy(bf16[16,40,4,128]{1,0,3,2:T(8,128)(2,1)S(1)} %bitcast.65) | data formatting | bytes 1966080 | tf_op jit(solution)/shard_map/convert_element_type | solution.py:90
  63.4 1.8 %convert_reduce_fusion.1 = f32[40,512]{0,1:T(8,128)} fusion(bf16[512,16,40]{2,1,0:T(8,128)(2,1)S(1)} %reshape.55), kind=kLoop, calls=%fused_computation.46 | loop fusion | flops 634880 | bytes 737280 | tf_op jit(solution)/shard_map/reduce_sum | solution.py:91
  65.3 1.0 reduce_sum.36
  66.6 11.9 %all-gather.2.cloned.1.call-done = bf16[64,20480]{1,0:T(8,128)(2,1)} async-done(((bf16[16,20480]{1,0:T(8,128)(2,1)}), bf16[64,20480]{1,0:T(8,128)(2,1)}) %all-gather.2.cloned.1.call-update) | async-done | bytes 2621456 | tf_op jit(solution)/shard_map/all_gather | solution.py:126
  78.4 2.4 %convert_reduce_fusion = f32[20480]{0:T(1024)S(1)} fusion(bf16[64,20480]{1,0:T(8,128)(2,1)} %all-gather.2.cloned.1.call-done), kind=kLoop, calls=%fused_computation.7 | loop fusion | flops 2600960 | bytes 2703360 | tf_op jit(solution)/shard_map/reduce_sum | solution.py:44
  81.4 1.0 fusion.9
  82.4 1.0 fusion.20
  83.4 1.0 fusion.23
  84.5 1.0 fusion.26
  85.5 1.6 %multiply_reduce_fusion = (f32[]{:T(128)}, f32[64,64]{1,0:T(8,128)S(1)}) fusion(f32[64,64]{1,0:T(8,128)S(1)} %fusion.26, f32[64,20480]{1,0:T(8,128)S(1)} %convert_subtract_fusion, f32[4096]{0:T(1024)S(1)} %get-tuple-element.72), kind=kOutput, calls=%fused_computation.65 | convolution fusion | flops 201617408 | bytes 2162692 | tf_op jit(solution)/shard_map/dot_general | solution.py:63
  88.0 2.1 %while.13 = (s32[]{:T(128)}, f32[64,64]{0,1:T(8,128)S(1)}, f32[64,64]{1,0:T(8,128)S(1)}, s32[]{:T(128)}) while((s32[]{:T(128)}, f32[64,64]{0,1:T(8,128)S(1)}, f32[64,64]{1,0:T(8,128)S(1)}, s32[]{:T(128)}) %tuple.38), condition=%wide.region_5.6_spmd.clone, body=%wide.region_4.5_spmd.clone.sunk | while | flops 9453570 | bytes 213045 | solution.py:82
  90.3 6.0 %fusion.39 = f32[64,1]{0,1:T(1,128)S(1)} fusion(f32[20480,1]{0,1:T(1,128)S(1)} %bitcast.74, bf16[64,20480]{1,0:T(8,128)(2,1)} %all-gather.2.cloned.1.call-done, f32[20480]{0:T(1024)S(1)} %get-tuple-element.77), kind=kOutput, calls=%fused_computation.39 | convolution fusion | flops 18350144 | bytes 2785536 | tf_op jit(solution)/shard_map/dot_general | solution.py:67
  96.4 1.4 %fusion.14 = bf16[64,40,128]{2,0,1:T(8,128)(2,1)S(1)} fusion(f32[64,40,128]{2,0,1:T(8,128)S(1)} %bitcast.66, f32[64,40,128]{2,0,1:T(8,128)S(1)} %bitcast_subtract_fusion, f32[40,128]{1,0:T(8,128)S(1)} %broadcast_multiply_fusion.1, pred[128]{0:T(512)(128)(4,1)S(1)} %copy-done.12, f32[64]{0:T(128)S(1)} %convolution_bitcast_fusion.2, ...), kind=kOutput, calls=%fused_computation.21 | convolution fusion | flops 252321792 | bytes 3314052 | tf_op jit(solution)/shard_map/isc,ij->jsc/dot_general | solution.py:93
  98.2 11.9 %all_to_all.27 = bf16[64,40,128]{2,1,0:T(8,128)(2,1)S(1)} all-to-all(bf16[64,40,128]{2,1,0:T(8,128)(2,1)S(1)} %copy.113), channel_id=1, replica_groups=mesh['mem'=4,'tile'=8] {'mem'}, dimensions={0} | all-to-all | bytes 1310720 | tf_op jit(solution)/shard_map/all_to_all | solution.py:140
  110.1 0.9 copy.125
  (79 shorter events, 6.9 us)
Async XLA Ops:
  7.8 0.7 copy-start.4
  7.8 0.7 copy-start.5
  7.9 1.1 copy-start.1
  7.9 1.1 copy-start.10
  9.0 0.8 copy-start.6
  9.5 0.7 copy-start.11
  28.2 2.5 %copy-start.7 = (s32[4096]{0:T(1024)S(1)}, s32[4096]{0:T(1024)}, u32[]{:S(2)}) copy-start(s32[4096]{0:T(1024)} %param.18) | copy-start | bytes 49156
  28.2 2.5 %copy-start.8 = (bf16[4096]{0:T(1024)(128)(2,1)S(1)}, bf16[4096]{0:T(1024)(128)(2,1)}, u32[]{:S(2)}) copy-start(bf16[4096]{0:T(1024)(128)(2,1)} %param.20) | copy-start | bytes 24580
  28.2 2.6 %copy-start.9 = (bf16[4096]{0:T(1024)(128)(2,1)S(1)}, bf16[4096]{0:T(1024)(128)(2,1)}, u32[]{:S(2)}) copy-start(bf16[4096]{0:T(1024)(128)(2,1)} %param.19) | copy-start | bytes 24580
  30.8 19.2 %collective-permute-start = (bf16[19,4096]{1,0:T(8,128)(2,1)S(1)}, bf16[19,4096]{1,0:T(8,128)(2,1)}, u32[]{:S(2)}, u32[]{:S(2)}) collective-permute-start(bf16[19,4096]{1,0:T(8,128)(2,1)S(1)} %pad_maximum_fusion), channel_id=1, source_target_pairs={{0,2},{1,3},{2,4},{3,5},{4,6},{5,7},{6,0},{7,1},{8,10},{9,11},{10,... | collective-permute-start | bytes 466952 | tf_op jit(solution)/shard_map/ppermute | solution.py:16
  33.0 18.0 %collective-permute-start.1 = (bf16[19,4096]{1,0:T(8,128)(2,1)S(1)}, bf16[19,4096]{1,0:T(8,128)(2,1)}, u32[]{:S(2)}, u32[]{:S(2)}) collective-permute-start(bf16[19,4096]{1,0:T(8,128)(2,1)S(1)} %pad_maximum_fusion), channel_id=1, source_target_pairs={{0,1},{1,2},{2,3},{3,4},{4,5},{5,6},{6,7},{7,0},{8,9},{9,10},{10,1... | collective-permute-start | bytes 466952 | tf_op jit(solution)/shard_map/ppermute | solution.py:16
  34.2 17.8 %collective-permute-start.2 = (bf16[19,4096]{1,0:T(8,128)(2,1)S(1)}, bf16[19,4096]{1,0:T(8,128)(2,1)S(1)}, u32[]{:S(2)}, u32[]{:S(2)}) collective-permute-start(bf16[19,4096]{1,0:T(8,128)(2,1)S(1)} %pad_maximum_fusion), channel_id=1, source_target_pairs={{0,7},{1,0},{2,1},{3,2},{4,3},{5,4},{6,5},{7,6},{8,15},{9,8},{10,9... | collective-permute-start | bytes 466952 | tf_op jit(solution)/shard_map/ppermute | solution.py:16
  37.2 14.9 %collective-permute-start.3 = (bf16[19,4096]{1,0:T(8,128)(2,1)S(1)}, bf16[19,4096]{1,0:T(8,128)(2,1)S(1)}, u32[]{:S(2)}, u32[]{:S(2)}) collective-permute-start(bf16[19,4096]{1,0:T(8,128)(2,1)S(1)} %pad_maximum_fusion), channel_id=1, source_target_pairs={{0,6},{1,7},{2,0},{3,1},{4,2},{5,3},{6,4},{7,5},{8,14},{9,15},{10,... | collective-permute-start | bytes 466952 | tf_op jit(solution)/shard_map/ppermute | solution.py:16
  43.8 14.2 %all-to-all-start = ((bf16[4,2,40960]{2,1,0:T(2,128)(2,1)}), bf16[4,2,40960]{2,1,0:T(2,128)(2,1)S(1)}, u32[]{:S(2)}, u32[]{:S(2)}) async-start(bf16[4,2,40960]{2,1,0:T(2,128)(2,1)} %reshape.54), calls=%async_computation | async-start | bytes 1310720 | tf_op jit(solution)/shard_map/all_to_all | solution.py:128
  48.8 29.6 %all-gather.2.cloned.1.call-start = ((), (), s32[]{:S(2)}) async-start(), calls=%async_computation.2 | async-start | bytes 3276800 | tf_op jit(solution)/shard_map/all_gather | solution.py:126
  66.5 14.3 %copy-start.2 = (f32[1,20480]{1,0:T(1,128)S(1)}, f32[1,20480]{1,0:T(1,128)}, u32[]{:S(2)}) copy-start(f32[1,20480]{1,0:T(1,128)} %fusion.50) | copy-start | bytes 245764
  66.5 14.3 %copy-start.3 = (f32[1,1,20480]{2,1,0:T(1,128)S(1)}, f32[1,1,20480]{2,1,0:T(1,128)}, u32[]{:S(2)}) copy-start(f32[1,1,20480]{2,1,0:T(1,128)} %param.21) | copy-start | bytes 245764
  78.4 2.5 %copy-start = (bf16[64,20480]{1,0:T(8,128)(2,1)S(1)}, bf16[64,20480]{1,0:T(8,128)(2,1)}, u32[]{:S(2)}) copy-start(bf16[64,20480]{1,0:T(8,128)(2,1)} %all-gather.2.cloned.1.call-done) | copy-start | bytes 7864324
  90.3 6.1 %copy-start.12 = (pred[128]{0:T(512)(128)(4,1)S(1)}, pred[128]{0:T(512)(128)(4,1)}, u32[]{:S(2)}) copy-start(pred[128]{0:T(512)(128)(4,1)} %dynamic-slice_compare_fusion) | copy-start | bytes 388
Sparse Core Ops, SparseCore 0:
  53.9 24.4 all-gather.1
where the time goes:
time: 119 us; the launch traced here: 118 us
  local copies, waits for them, and re-layouts  35.9 us (30%)
  waiting for transfers between devices  16.1 us (14%)
  matrix products  15.2 us (13%)
  between operations  14.5 us (12%)
  other arithmetic  12.4 us (10%)
  blocking collectives  11.9 us (10%)
  starting transfers between devices  11.6 us (10%)
    gather x1, local copies, waits for them, and re-layouts, measurement_operator(): return jnp.take(unrolled_ensemble, slot_index, axis=1)  14.2 us
    all_gather x1, waiting for transfers between devices, on_device(): everyone = lax.all_gather(nearby[:members_here], 'mem', axis=0, tiled=True)  11.9 us
    all_to_all x1, blocking collectives, on_device(): lax.all_to_all(outputs, 'mem', split_axis=0, concat_axis=2, tiled=True)  11.9 us
    unnamed x32, local copies, waits for them, and re-layouts  10.6 us
    ppermute x4, starting transfers between devices, from_behind(): return lax.ppermute(value, axis, pairs)  6.62 us
    dot_general x1, matrix products, weights_for(): jnp.dot(deviation, precision * innovation, precision=EXACT, preferred_ele...  5.97 us
    convert_element_type x2, local copies, waits for them, and re-layouts, vertical_mixing_step(): return result.astype(jnp.bfloat16)  5.78 us
    dot_general x5, matrix products, weights_for(): jnp.dot(scaled, portion.T, precision=EXACT, preferred_element_type=jnp.fl...  5.73 us
  transfers between devices with their start and end apart: 6, of which 2 were waited for; matrix products, arithmetic and copies ran while one was open for 17% of the time, Pallas kernels for 0%

commit v1 on v0

--- a/solution.py
+++ b/solution.py
@@ -1,6 +1,10 @@
+import functools
+
 import jax
 import jax.numpy as jnp
 from jax import lax
+from jax.experimental import pallas as pl
+from jax.experimental.pallas import tpu as pltpu
 from jax.sharding import PartitionSpec as P
 
 REACH = 2
@@ -95,7 +99,7 @@
     return result.astype(jnp.bfloat16)
 
 
-def on_device(
+def plain_on_device(
     ensemble_profiles_before,
     mixing_coefficient,
     surface_driver,
@@ -140,6 +144,393 @@
     return lax.all_to_all(outputs, "mem", split_axis=0, concat_axis=2, tiled=True)
 
 
+MESH = pl.DeviceIdType.MESH
+HALVES = 2
+FIELD_CUTS = (0.4, 0.7)
+CORES = 2
+
+
+def exact_dot(a, b):
+    return jnp.dot(a, b, precision=EXACT, preferred_element_type=jnp.float32)
+
+
+def kernel(
+    n_mem,
+    n_tile,
+    cuts,
+    ens_ref,
+    mix_ref,
+    surf_ref,
+    land_ref,
+    pos_ref,
+    field_ref,
+    valid_ref,
+    value_ref,
+    error_ref,
+    weight_ref,
+    out_ref,
+    fc_ref,
+    seen_ref,
+    near_ref,
+    rinv_ref,
+    part_ref,
+    got_ref,
+    tsend_ref,
+    trecv_ref,
+    moved_ref,
+    seen_send,
+    seen_recv,
+    fc_send,
+    fc_recv,
+    w_send,
+    w_recv,
+    p_send,
+    p_recv,
+    t_send,
+    t_recv,
+):
+    members, fields, columns = ens_ref.shape
+    everyone = members * n_mem
+    slots = pos_ref.shape[1]
+    near = 2 * REACH + 1
+    me, tile = lax.axis_index("mem"), lax.axis_index("tile")
+    n_y = n_mem // CORES
+    y, core = me // CORES, lax.rem(me, CORES)
+    sibling = y * CORES + (1 - core)
+    across = [lax.rem(y + step, n_y) * CORES + core for step in range(1, n_y)]
+    partner_of = [lax.rem(y + step, n_y) * CORES + (1 - core) for step in range(1, n_y)]
+
+    barrier = pltpu.get_barrier_semaphore()
+    for step in range(1, n_mem):
+        pl.semaphore_signal(
+            barrier, inc=1, device_id={"mem": lax.rem(me + step, n_mem)}, device_id_type=MESH
+        )
+    for offset in range(-REACH, REACH + 1):
+        if offset:
+            pl.semaphore_signal(
+                barrier,
+                inc=1,
+                device_id={"tile": lax.rem(tile + offset + n_tile, n_tile)},
+                device_id_type=MESH,
+            )
+
+    lanes = 128
+
+    def mix(step, carry):
+        where = pl.ds(pl.multiple_of(step * lanes, lanes), lanes)
+        x = jnp.transpose(ens_ref[:, :, where].astype(jnp.float32), (1, 0, 2))
+        rate = mix_ref[:, where][None]
+        above = jnp.concatenate([x[:1], x[:-1]], axis=0)
+        below = jnp.concatenate([x[1:], x[-1:]], axis=0)
+        stepped = x + rate * (above - 2.0 * x + below) - 0.05 * x * x * x
+        top = stepped[:1] + surf_ref[:, where][None]
+        stepped = jnp.concatenate([top, stepped[1:]], axis=0)
+        land = jnp.broadcast_to(land_ref[:, where][None], x.shape) > 0
+        fc_ref[me, :, :, where] = jnp.where(land, stepped, x).astype(jnp.bfloat16)
+        return carry
+
+    lax.fori_loop(0, columns // lanes, mix, 0)
+    pl.semaphore_wait(barrier, n_mem - 1 + 2 * REACH)
+
+    def remote(src, dst, send, recv, where):
+        return pltpu.make_async_remote_copy(
+            src_ref=src,
+            dst_ref=dst,
+            send_sem=send,
+            recv_sem=recv,
+            device_id=where,
+            device_id_type=MESH,
+        )
+
+    started = []
+
+    def go(copy):
+        copy.start()
+        started.append(copy)
+
+    def weight_copy(j):
+        return remote(
+            weight_ref.at[j],
+            near_ref.at[j],
+            w_send.at[j],
+            w_recv.at[j],
+            {"tile": lax.rem(tile + j - REACH + n_tile, n_tile)},
+        )
+
+    def fc_copy(q, owner, lane, target):
+        block = fc_ref.at[owner, pl.ds(cuts[q], cuts[q + 1] - cuts[q])]
+        return remote(block, block, fc_send.at[q, lane], fc_recv.at[q, owner], {"mem": target})
+
+    def seen_copy(h, owner, lane, target):
+        block = seen_ref.at[owner, h]
+        return remote(
+            block, block, seen_send.at[h, lane], seen_recv.at[h, owner], {"mem": target}
+        )
+
+    def own_fc(q):
+        for index, peer in enumerate(across):
+            go(fc_copy(q, me, index, peer))
+        go(fc_copy(q, me, n_y - 1, sibling))
+
+    def relay_fc(q):
+        for index, peer in enumerate(across):
+            fc_copy(q, peer, index, peer).wait_recv()
+            go(fc_copy(q, peer, n_y + index, sibling))
+
+    for j in range(near):
+        if j != REACH:
+            go(weight_copy(j))
+    own_fc(0)
+
+    half = slots // HALVES
+    width = min(half, 512)
+    for h in range(HALVES):
+
+        def pick(step, carry, h=h):
+            inner = pl.ds(pl.multiple_of(step * width, width), width)
+            where = pl.ds(pl.multiple_of(h * half + step * width, width), width)
+            rows = lax.broadcasted_iota(jnp.int32, (columns, width), 0)
+            hot = jnp.where(rows == pos_ref[:, where], 1.0, 0.0).astype(jnp.bfloat16)
+            flat = fc_ref[me].reshape(fields * members, columns)
+            found = jnp.dot(flat, hot, preferred_element_type=jnp.float32)
+            wanted = jnp.broadcast_to(field_ref[:, where], (members, width))
+            total = found[:members]
+            for f in range(1, fields):
+                total = jnp.where(wanted == f, found[f * members : (f + 1) * members], total)
+            seen_ref[me, h, :, inner] = total.astype(jnp.bfloat16)
+            return carry
+
+        lax.fori_loop(0, half // width, pick, 0)
+        for index, peer in enumerate(across):
+            go(seen_copy(h, me, index, peer))
+        go(seen_copy(h, me, n_y - 1, sibling))
+
+    n_cuts = len(cuts) - 1
+    for q in range(1, n_cuts):
+        own_fc(q)
+
+    base = valid_ref[...].astype(jnp.float32) / error_ref[...].astype(jnp.float32)
+    rinv_ref[...] = jnp.zeros_like(rinv_ref)
+    for j in range(near):
+        if j == REACH:
+            rinv_ref[j : j + 1, :] = base * weight_ref[j]
+        else:
+            weight_copy(j).wait_recv()
+            rinv_ref[j : j + 1, :] = base * near_ref[j]
+    part_ref[...] = jnp.zeros_like(part_ref)
+
+    for h in range(HALVES):
+        for index, peer in enumerate(across):
+            seen_copy(h, peer, index, peer).wait_recv()
+            go(seen_copy(h, peer, n_y + index, sibling))
+    for h in range(HALVES):
+        for owner in [sibling, *partner_of]:
+            seen_copy(h, owner, 0, sibling).wait_recv()
+
+        def gather_stats(step, carry, h=h):
+            inner = pl.ds(pl.multiple_of(step * width, width), width)
+            where = pl.ds(pl.multiple_of(h * half + step * width, width), width)
+            seen = jnp.concatenate(
+                [seen_ref[m, h, :, inner].astype(jnp.float32) for m in range(n_mem)], axis=0
+            )
+            average = jnp.mean(seen, axis=0, keepdims=True)
+            deviation = seen - average
+            innovation = value_ref[:, where].astype(jnp.float32) - average
+            rinv = rinv_ref[:, where]
+            high = deviation.astype(jnp.bfloat16)
+            low = (deviation - high.astype(jnp.float32)).astype(jnp.bfloat16)
+            right = jnp.concatenate([high, low], axis=0)
+            pulls = rinv * innovation
+            rows = [(deviation * rinv[j : j + 1]).astype(jnp.bfloat16) for j in range(near)]
+            rows.append(jnp.concatenate([pulls, jnp.zeros_like(pulls)], axis=0).astype(jnp.bfloat16))
+            left = jnp.concatenate(rows, axis=0)
+            sums = lax.dot_general(
+                left, right, (((1,), (1,)), ((), ())), preferred_element_type=jnp.float32
+            )
+            for j in range(near):
+                part_ref[j, :everyone] += sums[j * everyone : (j + 1) * everyone]
+                part_ref[j, everyone:] += jnp.broadcast_to(
+                    sums[near * everyone + j : near * everyone + j + 1], (8, 2 * everyone)
+                )
+            return carry
+
+        lax.fori_loop(0, half // width, gather_stats, 0)
+
+    def part_copy(j):
+        return remote(
+            part_ref.at[j],
+            got_ref.at[j],
+            p_send.at[j],
+            p_recv.at[j],
+            {"tile": lax.rem(tile - (j - REACH) + n_tile, n_tile)},
+        )
+
+    for j in range(near):
+        if j != REACH:
+            go(part_copy(j))
+    for q in range(n_cuts - 1):
+        relay_fc(q)
+    summed = part_ref[REACH]
+    for j in range(near):
+        if j != REACH:
+            part_copy(j).wait_recv()
+            summed = summed + got_ref[j]
+    summed = (summed[:, :everyone] + summed[:, everyone:]) / (everyone - 1.0)
+    rows = lax.broadcasted_iota(jnp.int32, (everyone, everyone), 0)
+    identity = jnp.where(
+        rows == lax.broadcasted_iota(jnp.int32, (everyone, everyone), 1), 1.0, 0.0
+    )
+    system = identity + summed[:everyone]
+    pulled = summed[everyone:]
+    scale = jnp.sqrt(jnp.sum(system * system, keepdims=True))
+    current = system / scale
+    root = 1.5 * identity - 0.5 * current
+    current = exact_dot(current, root)
+    for sweep in range(1, NS_ITERS):
+        middle = 1.5 * identity - 0.5 * exact_dot(root, current)
+        if sweep < NS_ITERS - 1:
+            current = exact_dot(current, middle)
+        root = exact_dot(middle, root)
+    root = root / jnp.sqrt(scale)
+    mean_weight = exact_dot(exact_dot(pulled, root), root)[:1]
+    turned = root + mean_weight
+    turned = turned + (1.0 - jnp.sum(turned, axis=1, keepdims=True)) / everyone
+    for m in range(n_mem):
+        tsend_ref[m, :, :everyone] = turned[m * members : (m + 1) * members]
+        tsend_ref[m, :, everyone:] = jnp.zeros((members, everyone), jnp.float32)
+
+    def t_copy(owner, target, lane):
+        return remote(
+            tsend_ref.at[target],
+            trecv_ref.at[owner],
+            t_send.at[lane],
+            t_recv.at[owner],
+            {"mem": target},
+        )
+
+    for step in range(1, n_mem):
+        go(t_copy(me, lax.rem(me + step, n_mem), step))
+    trecv_ref[me] = tsend_ref[me]
+    relay_fc(n_cuts - 1)
+    for q in range(n_cuts):
+        for owner in [sibling, *partner_of]:
+            fc_copy(q, owner, 0, sibling).wait_recv()
+    for step in range(1, n_mem):
+        t_copy(lax.rem(me + step, n_mem), me, step).wait_recv()
+
+    wide = columns // n_mem
+    group = 8
+
+    def apply(block, carry):
+        where = pl.ds(pl.multiple_of(block * wide, wide), wide)
+        weights = trecv_ref[block][:, :everyone]
+        high = weights.astype(jnp.bfloat16)
+        low = (weights - high.astype(jnp.float32)).astype(jnp.bfloat16)
+        left = jnp.concatenate([high, low], axis=0)
+        land = jnp.broadcast_to(land_ref[:, where], (members, wide)) > 0
+        for first in range(0, fields, group):
+            states = jnp.concatenate(
+                [
+                    jnp.concatenate([fc_ref[m, f, :, where] for m in range(n_mem)], axis=0)
+                    for f in range(first, first + group)
+                ],
+                axis=1,
+            )
+            both = jnp.dot(left, states, preferred_element_type=jnp.float32)
+            total = both[:members] + both[members:]
+            for f in range(group):
+                moved_ref[first + f, :, :] = jnp.where(
+                    land,
+                    total[:, f * wide : (f + 1) * wide],
+                    fc_ref[me, first + f, :, where].astype(jnp.float32),
+                )
+        out_ref[:, :, where] = jnp.transpose(moved_ref[...], (1, 0, 2)).astype(jnp.bfloat16)
+        return carry
+
+    lax.fori_loop(0, n_mem, apply, 0)
+    for copy in started:
+        copy.wait_send()
+
+
+def on_device(
+    n_mem,
+    n_tile,
+    ensemble_profiles_before,
+    mixing_coefficient,
+    surface_driver,
+    terrain_indicator,
+    measured_profile_position,
+    measured_field_index,
+    obs_valid,
+    obs_value,
+    obs_error,
+    local_weight,
+):
+    members, fields, columns = ensemble_profiles_before.shape
+    slots = measured_field_index.shape[0]
+    everyone = members * n_mem
+    near = 2 * REACH + 1
+    n_y = n_mem // CORES
+    cuts = (0, *[int(fields * cut) for cut in FIELD_CUTS], fields)
+    n_cuts = len(cuts) - 1
+    row = lambda a: a.reshape(1, -1)
+    whole = pl.BlockSpec(memory_space=pltpu.VMEM)
+    dma = pltpu.SemaphoreType.DMA
+    return pl.pallas_call(
+        functools.partial(kernel, n_mem, n_tile, cuts),
+        out_shape=jax.ShapeDtypeStruct(ensemble_profiles_before.shape, jnp.bfloat16),
+        in_specs=[whole] * 10,
+        out_specs=whole,
+        scratch_shapes=[
+            pltpu.VMEM((n_mem, fields, members, columns), jnp.bfloat16),
+            pltpu.VMEM((n_mem, HALVES, members, slots // HALVES), jnp.bfloat16),
+            pltpu.VMEM((near, 1, slots), jnp.float32),
+            pltpu.VMEM((8, slots), jnp.float32),
+            pltpu.VMEM((near, everyone + 8, 2 * everyone), jnp.float32),
+            pltpu.VMEM((near, everyone + 8, 2 * everyone), jnp.float32),
+            pltpu.VMEM((n_mem, members, 2 * everyone), jnp.float32),
+            pltpu.VMEM((n_mem, members, 2 * everyone), jnp.float32),
+            pltpu.VMEM((fields, members, columns // n_mem), jnp.float32),
+            dma((HALVES, 2 * n_y)),
+            dma((HALVES, n_mem)),
+            dma((n_cuts, 2 * n_y)),
+            dma((n_cuts, n_mem)),
+            dma((near,)),
+            dma((near,)),
+            dma((near,)),
+            dma((near,)),
+            dma((n_mem,)),
+            dma((n_mem,)),
+        ],
+        compiler_params=pltpu.CompilerParams(
+            collective_id=0, has_side_effects=True, vmem_limit_bytes=48 * 2**20
+        ),
+    )(
+        ensemble_profiles_before,
+        row(mixing_coefficient),
+        surface_driver,
+        row(terrain_indicator),
+        row(measured_profile_position),
+        row(measured_field_index),
+        row(obs_valid),
+        row(obs_value),
+        row(obs_error),
+        local_weight.reshape(near, 1, slots),
+    )
+
+
+def fits(n_mem, n_tile, ensemble, slots):
+    members, fields, columns = ensemble[0] // n_mem, ensemble[1], ensemble[2] // n_tile
+    return (
+        n_mem % CORES == 0
+        and n_tile > 2 * REACH
+        and members % 16 == 0
+        and fields % 8 == 0
+        and columns % (128 * n_mem) == 0
+        and slots // n_tile % (512 * HALVES) == 0
+    )
+
+
 def solution(mesh):
     in_specs = (
         P("mem", None, "tile"),
@@ -154,6 +545,14 @@
         P("mem", "tile", None),
     )
     out_specs = P("mem", None, "tile")
-    return jax.shard_map(
-        on_device, mesh=mesh, in_specs=in_specs, out_specs=out_specs, check_vma=False
-    )
+
+    def run(*args):
+        sizes = mesh.shape["mem"], mesh.shape["tile"]
+        body = plain_on_device
+        if fits(*sizes, args[0].shape, args[5].shape[0]):
+            body = functools.partial(on_device, *sizes)
+        return jax.shard_map(
+            body, mesh=mesh, in_specs=in_specs, out_specs=out_specs, check_vma=False
+        )(*args)
+
+    return run

time: 119 us -> 35.8 us (0.30)
  the two profiles are of different devices: /device:TPU:1 before, /device:TPU:0 now
where the time goes in v1:
time: 35.8 us; the launch traced here: 35.3 us
  Pallas kernels  29.5 us (82%)
  local copies, waits for them, and re-layouts  5.7 us (16%)
    pallas_call x1, Pallas kernels, on_device(): pl.pallas_call(functools.partial(kernel, n_mem, n_tile, cuts), out_shape=...  29.5 us
    unnamed x17, local copies, waits for them, and re-layouts  4.26 us
    reshape x2, local copies, waits for them, and re-layouts, on_device(): row = lambda a: a.reshape(1, -1)  1.44 us

profile of v1, /device:TPU:0, one launch (start us, length us, event | category | flops | bytes accessed | tf_op | source)
XLA Modules:
  0.0 35.3 jit_solution(4271166575371075010)
XLA Ops:
  0.0 0.0 copy-start.2
  0.0 0.7 %reshape.29.value_ref = bf16[1,4096]{1,0:T(2,128)(2,1)S(1)} reshape(bf16[4096]{0:T(1024)(128)(2,1)} %param.17) | data formatting | bytes 16384 | tf_op jit(solution)/shard_map/reshape | solution.py:476
  0.7 0.0 copy-start.3
  0.7 0.0 copy-start.6
  0.7 0.0 copy-start.7
  0.8 0.7 %reshape.30.error_ref = bf16[1,4096]{1,0:T(2,128)(2,1)S(1)} reshape(bf16[4096]{0:T(1024)(128)(2,1)} %param.18) | data formatting | bytes 16384 | tf_op jit(solution)/shard_map/reshape | solution.py:476
  1.5 0.0 copy-done.2
  1.5 0.0 copy-done.3
  1.5 0.0 copy-done.6
  1.5 0.0 copy-done.7
  1.5 0.0 copy-start
  1.5 1.1 %copy-done = bf16[16,40,512]{2,1,0:T(8,128)(2,1)S(1)} copy-done((bf16[16,40,512]{2,1,0:T(8,128)(2,1)S(1)}, bf16[16,40,512]{2,1,0:T(8,128)(2,1)}, u32[]{:S(2)}) %copy-start) | copy-done | bytes 655384
  2.6 0.0 copy-start.1
  2.6 0.9 %copy-done.1 = f32[1,1,20480]{2,1,0:T(1,128)S(1)} copy-done((f32[1,1,20480]{2,1,0:T(1,128)S(1)}, f32[1,1,20480]{2,1,0:T(1,128)}, u32[]{:S(2)}) %copy-start.1) | copy-done | bytes 81944
  3.5 0.0 copy-start.4
  3.5 0.7 %copy-done.4 = s32[4096]{0:T(1024)S(1)} copy-done((s32[4096]{0:T(1024)S(1)}, s32[4096]{0:T(1024)}, u32[]{:S(2)}) %copy-start.4) | copy-done | bytes 16408
  4.2 0.0 copy-start.5
  4.2 0.7 %copy-done.5 = s32[4096]{0:T(1024)S(1)} copy-done((s32[4096]{0:T(1024)S(1)}, s32[4096]{0:T(1024)}, u32[]{:S(2)}) %copy-start.5) | copy-done | bytes 16408
  4.9 29.5 %shard_map.100 = bf16[16,40,512]{2,1,0:T(8,128)(2,1)S(1)} custom-call(bf16[16,40,512]{2,1,0:T(8,128)(2,1)S(1)} %copy-done, f32[1,512]{1,0:T(1,128)S(1)} %bitcast.10, f32[16,512]{1,0:T(8,128)S(1)} %copy-done.2, s32[1,512]{1,0:T(1,128)S(1)} %bitcast.11, s32[1,4096]{1,0:T(1,128)S(1)} %bitcast.7, s32[1,4096]{1,0:T(1,128)S(1)} %bitcast.8, s32[1,4096]{1,0:T(1,128)S(1)} %bitcast.9, ...), custom_call_target="tpu_custom_call" | custom-call | tf_op jit(solution)/shard_map/pallas_call | solution.py:479
  34.5 0.8 %copy.12 = bf16[16,40,512]{2,1,0:T(8,128)(2,1)} copy(bf16[16,40,512]{2,1,0:T(8,128)(2,1)S(1)} %shard_map.100) | data formatting | bytes 1310720
Async XLA Ops:
  0.0 1.5 %copy-start.2 = (f32[16,512]{1,0:T(8,128)S(1)}, f32[16,512]{1,0:T(8,128)}, u32[]{:S(2)}) copy-start(f32[16,512]{1,0:T(8,128)} %surf_ref.1) | copy-start | bytes 98308
  0.7 0.8 %copy-start.3 = (s32[4096]{0:T(1024)S(1)}, s32[4096]{0:T(1024)}, u32[]{:S(2)}) copy-start(s32[4096]{0:T(1024)} %param.14) | copy-start | bytes 49156
  0.7 0.8 %copy-start.6 = (f32[512]{0:T(512)S(1)}, f32[512]{0:T(512)}, u32[]{:S(2)}) copy-start(f32[512]{0:T(512)} %param.11) | copy-start | bytes 6148
  0.7 0.8 %copy-start.7 = (s32[512]{0:T(512)S(1)}, s32[512]{0:T(512)}, u32[]{:S(2)}) copy-start(s32[512]{0:T(512)} %param.13) | copy-start | bytes 6148
  1.5 1.1 %copy-start = (bf16[16,40,512]{2,1,0:T(8,128)(2,1)S(1)}, bf16[16,40,512]{2,1,0:T(8,128)(2,1)}, u32[]{:S(2)}) copy-start(bf16[16,40,512]{2,1,0:T(8,128)(2,1)} %ens_ref.1) | copy-start | bytes 1966084
  2.6 0.9 %copy-start.1 = (f32[1,1,20480]{2,1,0:T(1,128)S(1)}, f32[1,1,20480]{2,1,0:T(1,128)}, u32[]{:S(2)}) copy-start(f32[1,1,20480]{2,1,0:T(1,128)} %param.19) | copy-start | bytes 245764
  3.5 0.7 %copy-start.4 = (s32[4096]{0:T(1024)S(1)}, s32[4096]{0:T(1024)}, u32[]{:S(2)}) copy-start(s32[4096]{0:T(1024)} %param.15) | copy-start | bytes 49156
  4.2 0.7 %copy-start.5 = (s32[4096]{0:T(1024)S(1)}, s32[4096]{0:T(1024)}, u32[]{:S(2)}) copy-start(s32[4096]{0:T(1024)} %param.16) | copy-start | bytes 49156

commit v2 on v1

--- a/solution.py
+++ b/solution.py
@@ -146,7 +146,7 @@
 
 MESH = pl.DeviceIdType.MESH
 HALVES = 2
-FIELD_CUTS = (0.4, 0.7)
+FIELD_CUTS = (0.15, 0.5, 0.8)
 CORES = 2
 
 
@@ -158,6 +158,17 @@
     n_mem,
     n_tile,
     cuts,
+    ens_hbm,
+    mix_hbm,
+    surf_hbm,
+    land_hbm,
+    pos_hbm,
+    field_hbm,
+    valid_hbm,
+    value_hbm,
+    error_hbm,
+    weight_hbm,
+    out_ref,
     ens_ref,
     mix_ref,
     surf_ref,
@@ -167,17 +178,18 @@
     valid_ref,
     value_ref,
     error_ref,
-    weight_ref,
-    out_ref,
     fc_ref,
     seen_ref,
     near_ref,
-    rinv_ref,
+    slot_ref,
+    acc_ref,
     part_ref,
     got_ref,
     tsend_ref,
     trecv_ref,
     moved_ref,
+    ens_sem,
+    in_sem,
     seen_send,
     seen_recv,
     fc_send,
@@ -216,8 +228,38 @@
 
     lanes = 128
 
+    def ens_copy(step):
+        where = pl.ds(pl.multiple_of(step * lanes, lanes), lanes)
+        return pltpu.make_async_copy(
+            ens_hbm.at[:, :, where], ens_ref.at[:, :, where], ens_sem.at[step]
+        )
+
+    pairs = [
+        (mix_hbm, mix_ref),
+        (surf_hbm, surf_ref),
+        (land_hbm, land_ref),
+        (pos_hbm, pos_ref),
+        (field_hbm, field_ref),
+        (valid_hbm, valid_ref),
+        (value_hbm, value_ref),
+        (error_hbm, error_ref),
+        (weight_hbm.at[REACH], near_ref.at[REACH]),
+    ]
+    inputs = [
+        pltpu.make_async_copy(src, dst, in_sem.at[index]) for index, (src, dst) in enumerate(pairs)
+    ]
+    for copy in inputs[:3]:
+        copy.start()
+    for step in range(columns // lanes):
+        ens_copy(step).start()
+    for copy in inputs[3:]:
+        copy.start()
+    for copy in inputs[:3]:
+        copy.wait()
+
     def mix(step, carry):
         where = pl.ds(pl.multiple_of(step * lanes, lanes), lanes)
+        ens_copy(step).wait()
         x = jnp.transpose(ens_ref[:, :, where].astype(jnp.float32), (1, 0, 2))
         rate = mix_ref[:, where][None]
         above = jnp.concatenate([x[:1], x[:-1]], axis=0)
@@ -250,7 +292,7 @@
 
     def weight_copy(j):
         return remote(
-            weight_ref.at[j],
+            weight_hbm.at[j],
             near_ref.at[j],
             w_send.at[j],
             w_recv.at[j],
@@ -282,6 +324,8 @@
             go(weight_copy(j))
     own_fc(0)
 
+    for copy in inputs[3:]:
+        copy.wait()
     half = slots // HALVES
     width = min(half, 512)
     for h in range(HALVES):
@@ -310,14 +354,15 @@
         own_fc(q)
 
     base = valid_ref[...].astype(jnp.float32) / error_ref[...].astype(jnp.float32)
-    rinv_ref[...] = jnp.zeros_like(rinv_ref)
+    slot_ref[near] = value_ref[...].astype(jnp.float32)
+    for spare in range(near + 1, slot_ref.shape[0]):
+        slot_ref[spare] = jnp.zeros_like(base)
     for j in range(near):
-        if j == REACH:
-            rinv_ref[j : j + 1, :] = base * weight_ref[j]
-        else:
+        if j != REACH:
             weight_copy(j).wait_recv()
-            rinv_ref[j : j + 1, :] = base * near_ref[j]
-    part_ref[...] = jnp.zeros_like(part_ref)
+        slot_ref[j] = base * near_ref[j]
+    acc_ref[...] = jnp.zeros_like(acc_ref)
+    relay_fc(0)
 
     for h in range(HALVES):
         for index, peer in enumerate(across):
@@ -329,14 +374,16 @@
 
         def gather_stats(step, carry, h=h):
             inner = pl.ds(pl.multiple_of(step * width, width), width)
-            where = pl.ds(pl.multiple_of(h * half + step * width, width), width)
             seen = jnp.concatenate(
                 [seen_ref[m, h, :, inner].astype(jnp.float32) for m in range(n_mem)], axis=0
             )
             average = jnp.mean(seen, axis=0, keepdims=True)
             deviation = seen - average
-            innovation = value_ref[:, where].astype(jnp.float32) - average
-            rinv = rinv_ref[:, where]
+            first = (h * half + step * width) // lanes
+            rinv = jnp.concatenate(
+                [slot_ref[:, first + r, :] for r in range(width // lanes)], axis=1
+            )
+            innovation = rinv[near : near + 1] - average
             high = deviation.astype(jnp.bfloat16)
             low = (deviation - high.astype(jnp.float32)).astype(jnp.bfloat16)
             right = jnp.concatenate([high, low], axis=0)
@@ -347,14 +394,19 @@
             sums = lax.dot_general(
                 left, right, (((1,), (1,)), ((), ())), preferred_element_type=jnp.float32
             )
-            for j in range(near):
-                part_ref[j, :everyone] += sums[j * everyone : (j + 1) * everyone]
-                part_ref[j, everyone:] += jnp.broadcast_to(
-                    sums[near * everyone + j : near * everyone + j + 1], (8, 2 * everyone)
-                )
+            acc_ref[...] += sums
             return carry
 
         lax.fori_loop(0, half // width, gather_stats, 0)
+
+    fold = everyone // 2
+    for j in range(near):
+        sums = acc_ref[j * everyone : (j + 1) * everyone]
+        sums = sums[:, :everyone] + sums[:, everyone:]
+        part_ref[j, :fold] = jnp.concatenate([sums[:fold], sums[fold:]], axis=1)
+        part_ref[j, fold:] = jnp.broadcast_to(
+            acc_ref[near * everyone + j : near * everyone + j + 1], (8, 2 * everyone)
+        )
 
     def part_copy(j):
         return remote(
@@ -368,20 +420,21 @@
     for j in range(near):
         if j != REACH:
             go(part_copy(j))
-    for q in range(n_cuts - 1):
+    for q in range(1, n_cuts - 2):
         relay_fc(q)
     summed = part_ref[REACH]
     for j in range(near):
         if j != REACH:
             part_copy(j).wait_recv()
             summed = summed + got_ref[j]
-    summed = (summed[:, :everyone] + summed[:, everyone:]) / (everyone - 1.0)
+    summed = summed / (everyone - 1.0)
+    spread = jnp.concatenate([summed[:fold, :everyone], summed[:fold, everyone:]], axis=0)
+    pulled = summed[fold:, :everyone] + summed[fold:, everyone:]
     rows = lax.broadcasted_iota(jnp.int32, (everyone, everyone), 0)
     identity = jnp.where(
         rows == lax.broadcasted_iota(jnp.int32, (everyone, everyone), 1), 1.0, 0.0
     )
-    system = identity + summed[:everyone]
-    pulled = summed[everyone:]
+    system = identity + spread
     scale = jnp.sqrt(jnp.sum(system * system, keepdims=True))
     current = system / scale
     root = 1.5 * identity - 0.5 * current
@@ -411,7 +464,8 @@
     for step in range(1, n_mem):
         go(t_copy(me, lax.rem(me + step, n_mem), step))
     trecv_ref[me] = tsend_ref[me]
-    relay_fc(n_cuts - 1)
+    for q in range(n_cuts - 2, n_cuts):
+        relay_fc(q)
     for q in range(n_cuts):
         for owner in [sibling, *partner_of]:
             fc_copy(q, owner, 0, sibling).wait_recv()
@@ -474,23 +528,36 @@
     cuts = (0, *[int(fields * cut) for cut in FIELD_CUTS], fields)
     n_cuts = len(cuts) - 1
     row = lambda a: a.reshape(1, -1)
-    whole = pl.BlockSpec(memory_space=pltpu.VMEM)
+    table = lambda a: a.reshape(-1, 128)
+    far = pl.BlockSpec(memory_space=pltpu.HBM)
     dma = pltpu.SemaphoreType.DMA
     return pl.pallas_call(
         functools.partial(kernel, n_mem, n_tile, cuts),
         out_shape=jax.ShapeDtypeStruct(ensemble_profiles_before.shape, jnp.bfloat16),
-        in_specs=[whole] * 10,
-        out_specs=whole,
+        in_specs=[far] * 10,
+        out_specs=pl.BlockSpec(memory_space=pltpu.VMEM),
         scratch_shapes=[
+            pltpu.VMEM((members, fields, columns), jnp.bfloat16),
+            pltpu.VMEM((1, columns), jnp.float32),
+            pltpu.VMEM((members, columns), jnp.float32),
+            pltpu.VMEM((1, columns), jnp.int32),
+            pltpu.VMEM((1, slots), jnp.int32),
+            pltpu.VMEM((1, slots), jnp.int32),
+            pltpu.VMEM((slots // 128, 128), jnp.int32),
+            pltpu.VMEM((slots // 128, 128), jnp.bfloat16),
+            pltpu.VMEM((slots // 128, 128), jnp.bfloat16),
             pltpu.VMEM((n_mem, fields, members, columns), jnp.bfloat16),
             pltpu.VMEM((n_mem, HALVES, members, slots // HALVES), jnp.bfloat16),
-            pltpu.VMEM((near, 1, slots), jnp.float32),
-            pltpu.VMEM((8, slots), jnp.float32),
-            pltpu.VMEM((near, everyone + 8, 2 * everyone), jnp.float32),
-            pltpu.VMEM((near, everyone + 8, 2 * everyone), jnp.float32),
+            pltpu.VMEM((near, slots // 128, 128), jnp.float32),
+            pltpu.VMEM((8, slots // 128, 128), jnp.float32),
+            pltpu.VMEM((near * everyone + 16, 2 * everyone), jnp.float32),
+            pltpu.VMEM((near, everyone // 2 + 8, 2 * everyone), jnp.float32),
+            pltpu.VMEM((near, everyone // 2 + 8, 2 * everyone), jnp.float32),
             pltpu.VMEM((n_mem, members, 2 * everyone), jnp.float32),
             pltpu.VMEM((n_mem, members, 2 * everyone), jnp.float32),
             pltpu.VMEM((fields, members, columns // n_mem), jnp.float32),
+            dma((columns // 128,)),
+            dma((9,)),
             dma((HALVES, 2 * n_y)),
             dma((HALVES, n_mem)),
             dma((n_cuts, 2 * n_y)),
@@ -512,10 +579,10 @@
         row(terrain_indicator),
         row(measured_profile_position),
         row(measured_field_index),
-        row(obs_valid),
-        row(obs_value),
-        row(obs_error),
-        local_weight.reshape(near, 1, slots),
+        table(obs_valid),
+        table(obs_value),
+        table(obs_error),
+        local_weight.reshape(near, slots // 128, 128),
     )
 
 

time: 35.8 us -> 36 us (level)
  the two profiles are of different devices: /device:TPU:0 before, /device:TPU:1 now
where the time goes in v2:
time: 36 us; the launch traced here: 35.4 us
  Pallas kernels  28.3 us (79%)
  local copies, waits for them, and re-layouts  7.12 us (20%)
    pallas_call x1, Pallas kernels, on_device(): pl.pallas_call(functools.partial(kernel, n_mem, n_tile, cuts), out_shape=...  28.3 us
    unnamed x21, local copies, waits for them, and re-layouts  7.12 us

profile of v2, /device:TPU:1, one launch (start us, length us, event | category | flops | bytes accessed | tf_op | source)
XLA Modules:
  0.0 35.4 jit_solution(8455182222779759747)
XLA Ops:
  0.0 0.0 copy-start.6
  0.0 0.0 copy-start.9
  0.0 0.0 copy-start.8
  0.0 0.7 %copy-done.6 = bf16[4096]{0:T(1024)(128)(2,1)S(1)} copy-done((bf16[4096]{0:T(1024)(128)(2,1)S(1)}, bf16[4096]{0:T(1024)(128)(2,1)}, u32[]{:S(2)}) %copy-start.6) | copy-done | bytes 8216
  0.7 0.0 copy-done.9
  0.7 0.0 copy-done.8
  0.7 0.0 copy-start
  0.7 1.1 %copy-done = bf16[16,40,512]{2,1,0:T(8,128)(2,1)S(1)} copy-done((bf16[16,40,512]{2,1,0:T(8,128)(2,1)S(1)}, bf16[16,40,512]{2,1,0:T(8,128)(2,1)}, u32[]{:S(2)}) %copy-start) | copy-done | bytes 655384
  1.8 0.0 copy-start.1
  1.8 0.9 %copy-done.1 = f32[1,1,20480]{2,1,0:T(1,128)S(1)} copy-done((f32[1,1,20480]{2,1,0:T(1,128)S(1)}, f32[1,1,20480]{2,1,0:T(1,128)}, u32[]{:S(2)}) %copy-start.1) | copy-done | bytes 81944
  2.7 0.0 copy-start.2
  2.7 0.8 %copy-done.2 = f32[16,512]{1,0:T(8,128)S(1)} copy-done((f32[16,512]{1,0:T(8,128)S(1)}, f32[16,512]{1,0:T(8,128)}, u32[]{:S(2)}) %copy-start.2) | copy-done | bytes 32792
  3.4 0.0 copy-start.3
  3.5 0.7 %copy-done.3 = s32[4096]{0:T(1024)S(1)} copy-done((s32[4096]{0:T(1024)S(1)}, s32[4096]{0:T(1024)}, u32[]{:S(2)}) %copy-start.3) | copy-done | bytes 16408
  4.2 0.0 copy-start.4
  4.2 0.7 %copy-done.4 = s32[4096]{0:T(1024)S(1)} copy-done((s32[4096]{0:T(1024)S(1)}, s32[4096]{0:T(1024)}, u32[]{:S(2)}) %copy-start.4) | copy-done | bytes 16408
  4.9 0.0 copy-start.5
  4.9 0.7 %copy-done.5 = s32[4096]{0:T(1024)S(1)} copy-done((s32[4096]{0:T(1024)S(1)}, s32[4096]{0:T(1024)}, u32[]{:S(2)}) %copy-start.5) | copy-done | bytes 16408
  5.6 0.0 copy-start.7
  5.6 0.7 %copy-done.7 = bf16[4096]{0:T(1024)(128)(2,1)S(1)} copy-done((bf16[4096]{0:T(1024)(128)(2,1)S(1)}, bf16[4096]{0:T(1024)(128)(2,1)}, u32[]{:S(2)}) %copy-start.7) | copy-done | bytes 8216
  6.3 28.3 %shard_map.100 = bf16[16,40,512]{2,1,0:T(8,128)(2,1)S(1)} custom-call(bf16[16,40,512]{2,1,0:T(8,128)(2,1)S(1)} %copy-done, f32[1,512]{1,0:T(1,128)S(1)} %bitcast.14, f32[16,512]{1,0:T(8,128)S(1)} %copy-done.2, s32[1,512]{1,0:T(1,128)S(1)} %bitcast.15, s32[1,4096]{1,0:T(1,128)S(1)} %bitcast.9, s32[1,4096]{1,0:T(1,128)S(1)} %bitcast.10, ...), custom_call_target="tpu_custom_call" | custom-call | tf_op jit(solution)/shard_map/pallas_call | solution.py:534
  34.6 0.8 %copy.12 = bf16[16,40,512]{2,1,0:T(8,128)(2,1)} copy(bf16[16,40,512]{2,1,0:T(8,128)(2,1)S(1)} %shard_map.100) | data formatting | bytes 1310720
Async XLA Ops:
  0.0 0.7 %copy-start.6 = (bf16[4096]{0:T(1024)(128)(2,1)S(1)}, bf16[4096]{0:T(1024)(128)(2,1)}, u32[]{:S(2)}) copy-start(bf16[4096]{0:T(1024)(128)(2,1)} %param.17) | copy-start | bytes 24580
  0.0 0.7 %copy-start.9 = (s32[512]{0:T(512)S(1)}, s32[512]{0:T(512)}, u32[]{:S(2)}) copy-start(s32[512]{0:T(512)} %param.13) | copy-start | bytes 6148
  0.0 0.7 %copy-start.8 = (f32[512]{0:T(512)S(1)}, f32[512]{0:T(512)}, u32[]{:S(2)}) copy-start(f32[512]{0:T(512)} %param.11) | copy-start | bytes 6148
  0.7 1.1 %copy-start = (bf16[16,40,512]{2,1,0:T(8,128)(2,1)S(1)}, bf16[16,40,512]{2,1,0:T(8,128)(2,1)}, u32[]{:S(2)}) copy-start(bf16[16,40,512]{2,1,0:T(8,128)(2,1)} %ens_hbm.1) | copy-start | bytes 1966084
  1.8 0.9 %copy-start.1 = (f32[1,1,20480]{2,1,0:T(1,128)S(1)}, f32[1,1,20480]{2,1,0:T(1,128)}, u32[]{:S(2)}) copy-start(f32[1,1,20480]{2,1,0:T(1,128)} %param.19) | copy-start | bytes 245764
  2.7 0.8 %copy-start.2 = (f32[16,512]{1,0:T(8,128)S(1)}, f32[16,512]{1,0:T(8,128)}, u32[]{:S(2)}) copy-start(f32[16,512]{1,0:T(8,128)} %surf_hbm.1) | copy-start | bytes 98308
  3.4 0.7 %copy-start.3 = (s32[4096]{0:T(1024)S(1)}, s32[4096]{0:T(1024)}, u32[]{:S(2)}) copy-start(s32[4096]{0:T(1024)} %param.14) | copy-start | bytes 49156
  4.2 0.7 %copy-start.4 = (s32[4096]{0:T(1024)S(1)}, s32[4096]{0:T(1024)}, u32[]{:S(2)}) copy-start(s32[4096]{0:T(1024)} %param.15) | copy-start | bytes 49156
  4.9 0.7 %copy-start.5 = (s32[4096]{0:T(1024)S(1)}, s32[4096]{0:T(1024)}, u32[]{:S(2)}) copy-start(s32[4096]{0:T(1024)} %param.16) | copy-start | bytes 49156
  5.6 0.7 %copy-start.7 = (bf16[4096]{0:T(1024)(128)(2,1)S(1)}, bf16[4096]{0:T(1024)(128)(2,1)}, u32[]{:S(2)}) copy-start(bf16[4096]{0:T(1024)(128)(2,1)} %param.18) | copy-start | bytes 24580

commit v3 on v2

--- a/solution.py
+++ b/solution.py
@@ -146,7 +146,7 @@
 
 MESH = pl.DeviceIdType.MESH
 HALVES = 2
-FIELD_CUTS = (0.15, 0.5, 0.8)
+FIELD_CUTS = (0.25, 0.5, 0.8)
 CORES = 2
 
 
@@ -533,7 +533,7 @@
     dma = pltpu.SemaphoreType.DMA
     return pl.pallas_call(
         functools.partial(kernel, n_mem, n_tile, cuts),
-        out_shape=jax.ShapeDtypeStruct(ensemble_profiles_before.shape, jnp.bfloat16),
+        out_shape=pltpu.VMEM(ensemble_profiles_before.shape, jnp.bfloat16),
         in_specs=[far] * 10,
         out_specs=pl.BlockSpec(memory_space=pltpu.VMEM),
         scratch_shapes=[
@@ -570,7 +570,7 @@
             dma((n_mem,)),
         ],
         compiler_params=pltpu.CompilerParams(
-            collective_id=0, has_side_effects=True, vmem_limit_bytes=48 * 2**20
+            collective_id=0, has_side_effects=True, vmem_limit_bytes=66_000_000
         ),
     )(
         ensemble_profiles_before,

time: 36 us -> 28.7 us (0.80); the launches traced: 35.4 us -> 28.6 us
  local copies, waits for them, and re-layouts: 7.12 us -> 0.84 us
  Pallas kernels: 28.3 us -> 27.7 us
    unnamed x21 -> x1, local copies, waits for them, and re-layouts: 7.12 us -> 0.84 us
    pallas_call x1, Pallas kernels: 28.3 us -> 27.7 us  [on_device(): pl.pallas_call(functools.partial(kernel, n_mem, n_tile, cuts), out_shape=...]
where the time goes in v3:
time: 28.7 us; the launch traced here: 28.6 us
  Pallas kernels  27.7 us (97%)
  local copies, waits for them, and re-layouts  0.84 us (3%)
    pallas_call x1, Pallas kernels, on_device(): pl.pallas_call(functools.partial(kernel, n_mem, n_tile, cuts), out_shape=...  27.7 us
    unnamed x1, local copies, waits for them, and re-layouts  0.84 us

profile of v3, /device:TPU:1, one launch (start us, length us, event | category | flops | bytes accessed | tf_op | source)
XLA Modules:
  0.0 28.6 jit_solution(10165739218721971493)
XLA Ops:
  0.0 27.7 %shard_map.100 = bf16[16,40,512]{2,1,0:T(8,128)(2,1)S(1)} custom-call(bf16[16,40,512]{2,1,0:T(8,128)(2,1)} %ens_hbm.1, f32[1,512]{1,0:T(1,128)} %bitcast.14, f32[16,512]{1,0:T(8,128)} %surf_hbm.1, s32[1,512]{1,0:T(1,128)} %bitcast.15, s32[1,4096]{1,0:T(1,128)} %bitcast.9, s32[1,4096]{1,0:T(1,128)} %bitcast.10, s32[32,128]{1,0:T(8,128)} %bitcast.11, ...), custom_call_target="tpu_custom_call" | custom-call | tf_op jit(solution)/shard_map/pallas_call | solution.py:534
  27.7 0.8 %copy.12 = bf16[16,40,512]{2,1,0:T(8,128)(2,1)} copy(bf16[16,40,512]{2,1,0:T(8,128)(2,1)S(1)} %shard_map.100) | data formatting | bytes 1310720
